TPU v7x, 32 devices: a whole 2x2x4 slice. The times are simulated.
32 devices in a mesh: group: 4 (over y, x), dp: 8 (over z, core).
Axes of the slice: x: 2, y: 2, z: 4, core: 2. Of those that a mesh axis runs over, the one named last changes fastest.
Arguments:
- observations: bfloat16 [64, 64, 4096], P('dp', None, 'group'), may hold values from -6 to 6
- next_observations: bfloat16 [1024, 4096], P('dp', 'group'), may hold values from -6 to 6
- trunk_weights: bfloat16 [2, 4096, 4096], P(None, 'dp', 'group'), may hold values from -0.125 to 0.125
- head_weights: bfloat16 [4096, 19], P('group'), may hold values from -0.25 to 0.25
- acting_policy_logits: float32 [64, 63, 18], P('dp'), may hold values from -16 to 330, as said below
- actions: int32 [64, 63], P('dp'), may hold values from 0 to 17
- rewards: float32 [64, 63], P('dp'), may hold values from -6 to 6
- episode_finished: int32 [64, 63], P('dp'), may hold values 0 or 1
Outputs:
- trunk_grads: float32 [2, 4096, 4096], P(None, 'dp', 'group')
- head_grads: float32 [4096, 19], P(('group', 'dp'))
- actor_logits: float32 [1024, 18], P('dp')
Inputs may be any that keep to these rules, and one draw needn't show every extreme that they name: `acting_policy_logits`: Real-valued scores, one row for each step and trajectory.
All inputs are finite; a program needn't handle non-finite values. No bound on the sum of `episode_finished` on one device may be relied on, other than what follows from the above.
Results may differ from a plain program's by a relative error of at most 0.012.
Values may be sent and summed in bfloat16 or wider, within the bound.
A program may use at most 128 MiB of HBM per device.

v0:
```python
import jax
import jax.numpy as jnp
from jax import lax
from jax.sharding import PartitionSpec as P

discount_rate = 0.99
value_weight = 0.5
entropy_weight = 0.1
loss_divisor = 16.0


def contract_rows(left, right):
    return lax.dot_general(
        left, right, (((0,), (0,)), ((), ())), preferred_element_type=jnp.float32
    )


def contract_cols(left, right):
    return lax.dot_general(
        left, right, (((1,), (1,)), ((), ())), preferred_element_type=jnp.float32
    )


def silu_slope(pre_value):
    sigma = jax.nn.sigmoid(pre_value)
    return sigma * (1.0 + pre_value * (1.0 - sigma))


def importance_trace_gradients(
    learner_output, acting_policy_logits, actions, rewards, episode_finished
):
    number_of_actions = acting_policy_logits.shape[-1]
    logits = learner_output[:, :, :number_of_actions]
    values = learner_output[:, :, number_of_actions]
    log_policy = jax.nn.log_softmax(logits[:, :-1], axis=-1)
    log_behave = jax.nn.log_softmax(acting_policy_logits, axis=-1)
    chosen = (
        actions[:, :, None] == jnp.arange(number_of_actions, dtype=jnp.int32)[None, None, :]
    ).astype(jnp.float32)
    ratio = jnp.exp(jnp.sum((log_policy - log_behave) * chosen, axis=-1))
    clipped = jnp.minimum(ratio, 1.0)
    discount = discount_rate * (1.0 - episode_finished.astype(jnp.float32))
    current = values[:, :-1]
    following = values[:, 1:]
    deltas = clipped * (rewards + discount * following - current)

    def backward_step(carried, step_item):
        delta_now, factor_now = step_item
        carried = delta_now + factor_now * carried
        return (carried, carried)

    start_carry = jnp.zeros((values.shape[0],), jnp.float32)
    _, corrections = lax.scan(
        backward_step, start_carry, (deltas.T, (discount * clipped).T), reverse=True
    )
    targets = current + corrections.T
    next_targets = jnp.concatenate([targets[:, 1:], values[:, -1:]], axis=1)
    advantage = clipped * (rewards + discount * next_targets - current)
    probability = jnp.exp(log_policy)
    entropy = -jnp.sum(probability * log_policy, axis=-1)
    logit_grad = (
        -advantage[..., None] * (chosen - probability)
        + entropy_weight * probability * (log_policy + entropy[..., None])
    ) / loss_divisor
    value_grad = -value_weight * (targets - current) / loss_divisor
    step_grad = jnp.concatenate([logit_grad, value_grad[..., None]], axis=-1)
    last_row = jnp.zeros((values.shape[0], 1, number_of_actions + 1), jnp.float32)
    return jnp.concatenate([step_grad, last_row], axis=1)


def per_device(
    observations,
    next_observations,
    trunk_weights,
    head_weights,
    acting_policy_logits,
    actions,
    rewards,
    episode_finished,
):
    traj_count, step_count, feature_block = observations.shape
    learner_rows = traj_count * step_count
    number_of_actions = acting_policy_logits.shape[-1]
    layer_total = trunk_weights.shape[0]
    own_rows = observations.reshape(learner_rows, feature_block)
    gathered_weights = [
        lax.all_gather(trunk_weights[layer_index], "dp", axis=0, tiled=True)
        for layer_index in range(layer_total)
    ]
    joined = jnp.concatenate([own_rows, next_observations], axis=0)
    inputs_full = []
    products_block = []
    current = joined
    for forward_layer_index in range(layer_total):
        forward_whole = lax.all_gather(current, "group", axis=1, tiled=True)
        inputs_full.append(forward_whole)
        product = jnp.dot(
            forward_whole, gathered_weights[forward_layer_index], preferred_element_type=jnp.float32
        )
        products_block.append(product)
        current = jax.nn.silu(product).astype(jnp.bfloat16)
    partial_head = jnp.dot(current, head_weights, preferred_element_type=jnp.float32)
    totals = lax.psum(partial_head, "group")
    inputs_full, products_block, last_block, totals = (inputs_full, products_block, current, totals)
    inputs_full = [whole[:learner_rows] for whole in inputs_full]
    products_block = [block[:learner_rows] for block in products_block]
    last_block = last_block[:learner_rows]
    head_out = totals[:learner_rows]
    actor_logits = totals[learner_rows:, :number_of_actions]
    learner_output = head_out.reshape(traj_count, step_count, number_of_actions + 1)
    output_gradient = importance_trace_gradients(
        learner_output, acting_policy_logits, actions, rewards, episode_finished
    )
    output_gradient = output_gradient.reshape(learner_rows, number_of_actions + 1).astype(
        jnp.bfloat16
    )
    head_partial = contract_rows(last_block, output_gradient)
    head_grads = lax.psum_scatter(head_partial, "dp", scatter_dimension=0, tiled=True)
    input_grad = contract_cols(output_gradient, head_weights)
    grad_list = [None] * layer_total
    for layer_index in range(layer_total - 1, -1, -1):
        pre_grad = (input_grad * silu_slope(products_block[layer_index])).astype(jnp.bfloat16)
        all_inputs = lax.all_to_all(
            inputs_full[layer_index], "dp", split_axis=1, concat_axis=0, tiled=True
        )
        all_upstream = lax.all_gather(pre_grad, "dp", axis=0, tiled=True)
        grad_list[layer_index] = contract_rows(all_inputs, all_upstream)
        if layer_index > 0:
            full_grad = contract_cols(pre_grad, gathered_weights[layer_index])
            input_grad = lax.psum_scatter(full_grad, "group", scatter_dimension=1, tiled=True)
    return (jnp.stack(grad_list), head_grads, actor_logits)


def solution(mesh):
    in_specs = (
        P("dp", None, "group"),
        P("dp", "group"),
        P(None, "dp", "group"),
        P("group", None),
        P("dp", None, None),
        P("dp", None),
        P("dp", None),
        P("dp", None),
    )
    out_specs = (P(None, "dp", "group"), P(("group", "dp"), None), P("dp", None))
    return jax.shard_map(
        per_device, mesh=mesh, in_specs=in_specs, out_specs=out_specs, check_vma=False
    )
```

profile of v0, /device:TPU:0, one launch (start us, length us, event | category | flops | bytes accessed | tf_op | source)
XLA Modules:
  0.0 727.3 jit_solution(5411754395285372085)
XLA Ops:
  7.2 2.6 pad_maximum_fusion.1
  9.9 1.5 fusion.27
  11.5 0.7 all-gather.19.cloned.1.call-update
  12.3 62.2 %all-gather.9.cloned.1.call-done = bf16[640,4096]{1,0:T(8,128)(2,1)} async-done(((bf16[640,1024]{1,0:T(8,128)(2,1)}), bf16[640,4096]{1,0:T(8,128)(2,1)}) %all-gather.9.cloned.1.call-update) | async-done | bytes 5242896 | tf_op jit(solution)/shard_map/all_gather | solution.py:95
  74.5 83.7 %all-gather.17.cloned.1.call-done = bf16[1,4096,1024]{2,1,0:T(8,128)(2,1)} async-done(((bf16[1,512,1024]{2,1,0:T(8,128)(2,1)}), bf16[1,4096,1024]{2,1,0:T(8,128)(2,1)}) %all-gather.17.cloned.1.call-update) | async-done | bytes 8388624 | tf_op jit(solution)/shard_map/all_gather | solution.py:87
  158.1 10.7 %multiply_convert_fusion.1 = (bf16[640,1024]{1,0:T(8,128)(2,1)}, f32[640,1024]{1,0:T(8,128)S(1)}) fusion(bf16[640,4096]{1,0:T(8,128)(2,1)} %all-gather.9.cloned.1.call-done, bf16[1,4096,1024]{2,1,0:T(8,128)(2,1)} %all-gather.17.cloned.1.call-done), kind=kOutput, calls=%fused_computation.12 | convolution fusion | flops 5371985920 | bytes 17563648 | tf_op jit(solution)/shard_map/dot_general | solution.py:97
  169.1 71.2 %all-gather.19.cloned.1.call-done = bf16[1,4096,1024]{2,1,0:T(8,128)(2,1)} async-done(((bf16[1,512,1024]{2,1,0:T(8,128)(2,1)}), bf16[1,4096,1024]{2,1,0:T(8,128)(2,1)}) %all-gather.19.cloned.1.call-update) | async-done | bytes 8388624 | tf_op jit(solution)/shard_map/all_gather | solution.py:87
  240.3 62.1 %all-gather.11.cloned.1.call-done = bf16[640,4096]{1,0:T(8,128)(2,1)} async-done(((bf16[640,1024]{1,0:T(8,128)(2,1)}), bf16[640,4096]{1,0:T(8,128)(2,1)}) %all-gather.11.cloned.1.call-update) | async-done | bytes 5242896 | tf_op jit(solution)/shard_map/all_gather | solution.py:95
  302.4 10.9 %multiply_convert_fusion = (bf16[640,1024]{1,0:T(8,128)(2,1)S(1)}, f32[640,1024]{1,0:T(8,128)}) fusion(bf16[640,4096]{1,0:T(8,128)(2,1)} %all-gather.11.cloned.1.call-done, bf16[1,4096,1024]{2,1,0:T(8,128)(2,1)} %all-gather.19.cloned.1.call-done), kind=kOutput, calls=%fused_computation.11 | convolution fusion | flops 5371985920 | bytes 17563648 | tf_op jit(solution)/shard_map/dot_general | solution.py:97
  313.3 1.1 copy-done.3
  314.8 16.2 %psum.7 = f32[640,19]{0,1:T(8,128)S(1)} all-reduce(f32[640,19]{0,1:T(8,128)S(1)} %fusion.28), channel_id=1, replica_groups=mesh['group'=4,'dp'=8] {'group'}, use_global_device_ids=true, to_apply=%region_0.1 | all-reduce | flops 12160 | bytes 97280 | tf_op jit(solution)/shard_map/psum | solution.py:103
  331.5 4.7 while.17
  336.7 3.4 multiply_convert_fusion.3
  340.1 11.5 %fusion.2 = f32[512,4096]{1,0:T(8,128)} fusion(bf16[512,1024]{1,0:T(8,128)(2,1)} %multiply_convert_fusion.3, bf16[1,4096,1024]{2,1,0:T(8,128)(2,1)} %all-gather.19.cloned.1.call-done), kind=kOutput, calls=%fused_computation.3 | convolution fusion | flops 4294967296 | bytes 17825792 | tf_op jit(solution)/shard_map/dot_general | solution.py:19
  352.3 4.7 slice.62
  357.0 6.6 copy.47
  363.6 4.6 all-to-all-start
  368.4 69.6 %reduce-scatter.3.cloned.1.call-done = f32[512,1024]{1,0:T(8,128)} async-done(((f32[512,4096]{1,0:T(8,128)}), f32[512,1024]{1,0:T(8,128)}) %reduce-scatter.3.cloned.1.call-update) | async-done | bytes 2097168 | tf_op jit(solution)/shard_map/reduce_scatter | solution.py:130
  438.0 3.3 multiply_convert_fusion.2
  441.3 2.2 slice-done
  443.5 2.4 copy.55
  445.9 50.0 %all-to-all-done = bf16[512,8,512]{0,2,1:T(8,128)(2,1)} async-done(((bf16[512,8,512]{0,2,1:T(8,128)(2,1)}), bf16[512,8,512]{0,2,1:T(8,128)(2,1)}, u32[]{:S(2)}, u32[]{:S(2)}) %all-to-all-start) | async-done | bytes 4194336 | tf_op jit(solution)/shard_map/all_to_all | solution.py:123
  495.9 4.6 all-to-all-start.1
  500.5 6.6 copy.48
  507.2 0.6 slice.70
  507.8 0.9 fusion.8
  508.7 146.3 %all-to-all-done.1 = bf16[512,8,512]{2,0,1:T(8,128)(2,1)} async-done(((bf16[512,8,512]{2,0,1:T(8,128)(2,1)}), bf16[512,8,512]{2,0,1:T(8,128)(2,1)}, u32[]{:S(2)}, u32[]{:S(2)}) %all-to-all-start.1) | async-done | bytes 4194336 | tf_op jit(solution)/shard_map/all_to_all | solution.py:123
  655.0 8.3 %convolution_bitcast_fusion = f32[1,512,1024]{2,1,0:T(8,128)S(1)} fusion(bf16[4096,512]{1,0:T(8,128)(2,1)} %bitcast.13, bf16[4096,1024]{1,0:T(8,128)(2,1)} %all-gather.15.cloned.1.call-done), kind=kOutput, calls=%fused_computation.15 | convolution fusion | flops 4294967296 | bytes 14680064 | tf_op jit(solution)/shard_map/dot_general | solution.py:13
  663.3 26.0 %all-gather.13.cloned.1.call-done = bf16[4096,1024]{1,0:T(8,128)(2,1)} async-done(((bf16[512,1024]{1,0:T(8,128)(2,1)}), bf16[4096,1024]{1,0:T(8,128)(2,1)}) %all-gather.13.cloned.1.call-update) | async-done | bytes 8388624 | tf_op jit(solution)/shard_map/all_gather | solution.py:126
  689.3 8.2 %convolution_bitcast_fusion.1 = f32[1,512,1024]{2,1,0:T(8,128)S(1)} fusion(bf16[4096,512]{1,0:T(8,128)(2,1)} %bitcast.68, bf16[4096,1024]{1,0:T(8,128)(2,1)} %all-gather.13.cloned.1.call-done), kind=kOutput, calls=%fused_computation.16 | convolution fusion | flops 4294967296 | bytes 14680064 | tf_op jit(solution)/shard_map/dot_general | solution.py:13
  697.5 2.5 pad_maximum_fusion
  700.0 20.5 %reduce-scatter.5.cloned.1.call-done = f32[128,19]{0,1:T(8,128)} async-done(((f32[1024,19]{0,1:T(8,128)}), f32[128,19]{0,1:T(8,128)}) %reduce-scatter.5.cloned.1.call-update) | async-done | bytes 9744 | tf_op jit(solution)/shard_map/reduce_scatter | solution.py:118
  (185 shorter events, 6.3 us)
Async XLA Ops:
  7.2 307.2 %copy-start = (bf16[1024,19]{0,1:T(8,128)(2,1)S(1)}, bf16[1024,19]{0,1:T(8,128)(2,1)}, u32[]{:S(2)}) copy-start(bf16[1024,19]{0,1:T(8,128)(2,1)} %param.14) | copy-start | bytes 116740
  7.2 2.7 copy-start.2
  7.2 67.3 %all-gather.9.cloned.1.call-start = ((), (), s32[]{:S(2)}) async-start(), calls=%async_computation.4 | async-start | bytes 6553600 | tf_op jit(solution)/shard_map/all_gather | solution.py:95
  9.9 148.3 %all-gather.17.cloned.1.call-start = ((), (), s32[]{:S(2)}) async-start(), calls=%async_computation.10 | async-start | bytes 9437184 | tf_op jit(solution)/shard_map/all_gather | solution.py:87
  11.5 228.8 %all-gather.19.cloned.1.call-start = ((), (), s32[]{:S(2)}) async-start(), calls=%async_computation.11 | async-start | bytes 9437184 | tf_op jit(solution)/shard_map/all_gather | solution.py:87
  12.2 156.8 %copy-start.5 = (f32[8,63,18]{1,0,2:T(8,128)S(1)}, f32[8,63,18]{1,0,2:T(8,128)}, u32[]{:S(2)}) copy-start(f32[8,63,18]{1,0,2:T(8,128)} %param.15) | copy-start | bytes 108868
  12.2 290.2 %all-gather.11.cloned.1.call-start = ((), (), s32[]{:S(2)}) async-start(), calls=%async_computation.5 | async-start | bytes 6553600 | tf_op jit(solution)/shard_map/all_gather | solution.py:95
  168.9 269.1 %reduce-scatter.3.cloned.1.call-start = ((), (), s32[]{:S(2)}) async-start(), calls=%async_computation.6 | async-start | bytes 10485760 | tf_op jit(solution)/shard_map/reduce_scatter | solution.py:130
  169.0 162.1 %copy-start.8 = (s32[8,63]{1,0:T(8,128)S(1)}, s32[8,63]{1,0:T(8,128)}, u32[]{:S(2)}) copy-start(s32[8,63]{1,0:T(8,128)} %param.16) | copy-start | bytes 6052
  169.0 162.2 %copy-start.6 = (s32[8,63]{1,0:T(8,128)S(1)}, s32[8,63]{1,0:T(8,128)}, u32[]{:S(2)}) copy-start(s32[8,63]{1,0:T(8,128)} %param.18) | copy-start | bytes 6052
  169.0 162.2 %copy-start.7 = (f32[8,63]{1,0:T(8,128)S(1)}, f32[8,63]{1,0:T(8,128)}, u32[]{:S(2)}) copy-start(f32[8,63]{1,0:T(8,128)} %param.17) | copy-start | bytes 6052
  313.3 1.1 copy-start.3
  351.7 303.3 %all-gather.15.cloned.1.call-start = ((), (), s32[]{:S(2)}) async-start(), calls=%async_computation.8 | async-start | bytes 9437184 | tf_op jit(solution)/shard_map/all_gather | solution.py:126
  363.6 132.3 %all-to-all-start = ((bf16[512,8,512]{0,2,1:T(8,128)(2,1)}), bf16[512,8,512]{0,2,1:T(8,128)(2,1)}, u32[]{:S(2)}, u32[]{:S(2)}) async-start(bf16[512,8,512]{0,2,1:T(8,128)(2,1)} %bitcast.65), calls=%async_computation | async-start | bytes 8388608 | tf_op jit(solution)/shard_map/all_to_all | solution.py:123
  368.2 321.1 %all-gather.13.cloned.1.call-start = ((), (), s32[]{:S(2)}) async-start(), calls=%async_computation.7 | async-start | bytes 9437184 | tf_op jit(solution)/shard_map/all_gather | solution.py:126
  441.3 2.2 slice-start
  495.9 159.1 %all-to-all-start.1 = ((bf16[512,8,512]{2,0,1:T(8,128)(2,1)}), bf16[512,8,512]{2,0,1:T(8,128)(2,1)}, u32[]{:S(2)}, u32[]{:S(2)}) async-start(bf16[512,8,512]{2,0,1:T(8,128)(2,1)} %bitcast.66), calls=%async_computation.2 | async-start | bytes 8388608 | tf_op jit(solution)/shard_map/all_to_all | solution.py:123
  500.5 220.0 %reduce-scatter.5.cloned.1.call-start = ((), (), s32[]{:S(2)}) async-start(), calls=%async_computation.9 | async-start | bytes 110592 | tf_op jit(solution)/shard_map/reduce_scatter | solution.py:118
  500.5 7.3 copy-start.4
  689.3 31.2 %copy-start.1 = (bf16[1024,19]{0,1:T(8,128)(2,1)S(1)}, bf16[1024,19]{0,1:T(8,128)(2,1)}, u32[]{:S(2)}) copy-start(bf16[1024,19]{0,1:T(8,128)(2,1)} %param.14) | copy-start | bytes 116740
Sparse Core Ops, SparseCore 0:
  10.4 64.0 all-gather.8
  76.1 82.0 all-gather.16
  159.7 80.5 all-gather.18
  242.6 59.7 all-gather.10
  351.8 86.1 reduce-scatter.2
  439.4 153.6 all-gather.14
  594.7 94.5 all-gather.12
  692.1 28.3 reduce-scatter.4
where the time goes:
time: 728 us; the launch traced here: 727 us
  waiting for transfers between devices  593 us (81%)
  matrix products  54.4 us (7%)
  local copies, waits for them, and re-layouts  28.9 us (4%)
  blocking collectives  16.2 us (2%)
  between operations  14.3 us (2%)
  other arithmetic  9.97 us (1%)
  starting transfers between devices  9.68 us (1%)
    all_to_all x2, waiting for transfers between devices, per_device(): lax.all_to_all(inputs_full[layer_index], 'dp', split_axis=1, concat_axis=...  196 us
    all_gather x2, waiting for transfers between devices, per_device(): lax.all_gather(trunk_weights[layer_index], 'dp', axis=0, tiled=True)  155 us
    all_gather x2, waiting for transfers between devices, per_device(): forward_whole = lax.all_gather(current, 'group', axis=1, tiled=True)  124 us
    reduce_scatter x1, waiting for transfers between devices, per_device(): lax.psum_scatter(full_grad, 'group', scatter_dimension=1, tiled=True)  69.6 us
    all_gather x2, waiting for transfers between devices, per_device(): all_upstream = lax.all_gather(pre_grad, 'dp', axis=0, tiled=True)  26 us
    dot_general x2, matrix products, per_device(): jnp.dot(forward_whole, gathered_weights[forward_layer_index], preferred_e...  21.6 us
    reduce_scatter x1, waiting for transfers between devices, per_device(): lax.psum_scatter(head_partial, 'dp', scatter_dimension=0, tiled=True)  20.5 us
    dot_general x3, matrix products, contract_rows(): lax.dot_general(left, right, (((0,), (0,)), ((), ())), preferred_element_...  17.4 us
  transfers between devices with their start and end apart: 10, of which 9 were waited for; matrix products, arithmetic and copies ran while one was open for 8% of the time, Pallas kernels for 0%

commit v1 on v0

--- a/solution.py
+++ b/solution.py
@@ -84,7 +84,12 @@
     layer_total = trunk_weights.shape[0]
     own_rows = observations.reshape(learner_rows, feature_block)
     gathered_weights = [
-        lax.all_gather(trunk_weights[layer_index], "dp", axis=0, tiled=True)
+        jnp.concatenate(
+            lax.all_to_all(
+                jnp.stack([trunk_weights[layer_index]] * lax.axis_size("dp")), "dp", 0, 0
+            ),
+            axis=0,
+        )
         for layer_index in range(layer_total)
     ]
     joined = jnp.concatenate([own_rows, next_observations], axis=0)

time: 728 us -> 823 us (1.13)
  waiting for transfers between devices: 593 us -> 667 us
  starting transfers between devices: 9.68 us -> 20.9 us
  local copies, waits for them, and re-layouts: 28.9 us -> 37.7 us
    all_to_all x0 -> x2, waiting for transfers between devices: none -> 356 us  [per_device(): lax.all_to_all(jnp.stack([trunk_weights[layer_index]] * lax.axis_size('dp...]
    all_gather x2 -> x0, waiting for transfers between devices: 155 us -> none  [per_device(): lax.all_gather(trunk_weights[layer_index], 'dp', axis=0, tiled=True)]
    all_gather x2, waiting for transfers between devices: 124 us -> 0.02 us  [per_device(): forward_whole = lax.all_gather(current, 'group', axis=1, tiled=True)]
    all_to_all x2, waiting for transfers between devices: 196 us -> 209 us  [per_device(): lax.all_to_all(inputs_full[layer_index], 'dp', split_axis=1, concat_axis=...]
    all_to_all x0 -> x2, starting transfers between devices: none -> 11.4 us  [per_device(): lax.all_to_all(jnp.stack([trunk_weights[layer_index]] * lax.axis_size('dp...]
    all_gather x2, waiting for transfers between devices: 26 us -> 15.6 us  [per_device(): all_upstream = lax.all_gather(pre_grad, 'dp', axis=0, tiled=True)]
    another operation x0 -> x2, local copies, waits for them, and re-layouts: none -> 8.63 us  [per_device(): jnp.stack([trunk_weights[layer_index]] * lax.axis_size('dp'))]
  transfers between devices with their start and end apart: 10 -> 10, of which waited for: 9 -> 7; matrix products, arithmetic and copies ran while one was open for 8% -> 7% of each run, Pallas kernels for 0% -> 0%
where the time goes in v1:
time: 823 us; the launch traced here: 822 us
  waiting for transfers between devices  667 us (81%)
  matrix products  54.5 us (7%)
  local copies, waits for them, and re-layouts  37.7 us (5%)
  starting transfers between devices  20.9 us (3%)
  blocking collectives  17.2 us (2%)
  between operations  14.3 us (2%)
  other arithmetic  8.51 us (1%)
    all_to_all x2, waiting for transfers between devices, per_device(): lax.all_to_all(jnp.stack([trunk_weights[layer_index]] * lax.axis_size('dp...  356 us
    all_to_all x2, waiting for transfers between devices, per_device(): lax.all_to_all(inputs_full[layer_index], 'dp', split_axis=1, concat_axis=...  209 us
    reduce_scatter x1, waiting for transfers between devices, per_device(): lax.psum_scatter(full_grad, 'group', scatter_dimension=1, tiled=True)  66.9 us
    dot_general x2, matrix products, per_device(): jnp.dot(forward_whole, gathered_weights[forward_layer_index], preferred_e...  21.7 us
    reduce_scatter x1, waiting for transfers between devices, per_device(): lax.psum_scatter(head_partial, 'dp', scatter_dimension=0, tiled=True)  19.7 us
    dot_general x3, matrix products, contract_rows(): lax.dot_general(left, right, (((0,), (0,)), ((), ())), preferred_element_...  17.5 us
    psum x1, blocking collectives, per_device(): totals = lax.psum(partial_head, 'group')  17.2 us
  transfers between devices with their start and end apart: 10, of which 7 were waited for; matrix products, arithmetic and copies ran while one was open for 7% of the time, Pallas kernels for 0%

profile of v1, /device:TPU:0, one launch (start us, length us, event | category | flops | bytes accessed | tf_op | source)
XLA Modules:
  0.0 821.7 jit_solution(2879486630404839702)
XLA Ops:
  7.2 1.7 slice_bitcast_fusion
  8.9 4.3 stack.15
  13.2 6.5 all-to-all-start.1
  19.8 1.2 pad_maximum_fusion.1
  20.9 182.7 %all-to-all-done.1 = bf16[8,512,1024]{2,1,0:T(8,128)(2,1)} async-done(((bf16[8,512,1024]{2,1,0:T(8,128)(2,1)}), bf16[8,512,1024]{2,1,0:T(8,128)(2,1)}, u32[]{:S(2)}, u32[]{:S(2)}) %all-to-all-start.1) | async-done | bytes 8388640 | tf_op jit(solution)/shard_map/all_to_all | solution.py:88
  203.7 4.3 stack.16
  208.0 5.0 all-to-all-start.2
  213.0 10.8 %multiply_convert_fusion.1 = (bf16[640,1024]{1,0:T(8,128)(2,1)}, f32[640,1024]{1,0:T(8,128)S(1)}) fusion(bf16[640,4096]{1,0:T(8,128)(2,1)} %all-gather.5.cloned.1.call-done, bf16[4096,1024]{1,0:T(8,128)(2,1)} %bitcast.5), kind=kOutput, calls=%fused_computation.6 | convolution fusion | flops 5371985920 | bytes 17563648 | tf_op jit(solution)/shard_map/dot_general | solution.py:102
  224.0 172.8 %all-to-all-done.2 = bf16[8,512,1024]{2,1,0:T(8,128)(2,1)} async-done(((bf16[8,512,1024]{2,1,0:T(8,128)(2,1)}), bf16[8,512,1024]{2,1,0:T(8,128)(2,1)}, u32[]{:S(2)}, u32[]{:S(2)}) %all-to-all-start.2) | async-done | bytes 8388640 | tf_op jit(solution)/shard_map/all_to_all | solution.py:88
  396.8 10.9 %multiply_convert_fusion = (bf16[640,1024]{1,0:T(8,128)(2,1)S(1)}, f32[640,1024]{1,0:T(8,128)}) fusion(bf16[640,4096]{1,0:T(8,128)(2,1)} %all-gather.7.cloned.1.call-done, bf16[4096,1024]{1,0:T(8,128)(2,1)} %bitcast.7), kind=kOutput, calls=%fused_computation.5 | convolution fusion | flops 5371985920 | bytes 17563648 | tf_op jit(solution)/shard_map/dot_general | solution.py:102
  407.7 1.1 copy-done.2
  409.2 17.2 %psum.7 = f32[640,19]{0,1:T(8,128)S(1)} all-reduce(f32[640,19]{0,1:T(8,128)S(1)} %fusion.21), channel_id=1, replica_groups=mesh['group'=4,'dp'=8] {'group'}, use_global_device_ids=true, to_apply=%region_0.1 | all-reduce | flops 12160 | bytes 97280 | tf_op jit(solution)/shard_map/psum | solution.py:108
  427.0 4.7 while.17
  432.2 3.5 multiply_convert_fusion.3
  435.6 11.5 %fusion.22 = f32[512,4096]{1,0:T(8,128)} fusion(bf16[512,1024]{1,0:T(8,128)(2,1)} %multiply_convert_fusion.3, bf16[4096,1024]{1,0:T(8,128)(2,1)} %bitcast.7), kind=kOutput, calls=%fused_computation.52 | convolution fusion | flops 4294967296 | bytes 17825792 | tf_op jit(solution)/shard_map/dot_general | solution.py:19
  447.7 4.7 slice.68
  452.4 6.6 copy.47
  459.0 4.6 all-to-all-start
  463.7 66.9 %reduce-scatter.3.cloned.1.call-done = f32[512,1024]{1,0:T(8,128)} async-done(((f32[512,4096]{1,0:T(8,128)}), f32[512,1024]{1,0:T(8,128)}) %reduce-scatter.3.cloned.1.call-update) | async-done | bytes 2097168 | tf_op jit(solution)/shard_map/reduce_scatter | solution.py:135
  530.5 3.3 multiply_convert_fusion.2
  533.9 2.2 slice-done
  536.1 2.4 copy.55
  538.5 55.4 %all-to-all-done = bf16[512,8,512]{0,2,1:T(8,128)(2,1)} async-done(((bf16[512,8,512]{0,2,1:T(8,128)(2,1)}), bf16[512,8,512]{0,2,1:T(8,128)(2,1)}, u32[]{:S(2)}, u32[]{:S(2)}) %all-to-all-start) | async-done | bytes 4194336 | tf_op jit(solution)/shard_map/all_to_all | solution.py:128
  593.9 4.6 all-to-all-start.3
  598.6 6.7 copy.48
  605.9 0.9 fusion.2
  606.8 153.7 %all-to-all-done.3 = bf16[512,8,512]{2,0,1:T(8,128)(2,1)} async-done(((bf16[512,8,512]{2,0,1:T(8,128)(2,1)}), bf16[512,8,512]{2,0,1:T(8,128)(2,1)}, u32[]{:S(2)}, u32[]{:S(2)}) %all-to-all-start.3) | async-done | bytes 4194336 | tf_op jit(solution)/shard_map/all_to_all | solution.py:128
  760.5 8.4 %convolution_bitcast_fusion = f32[1,512,1024]{2,1,0:T(8,128)S(1)} fusion(bf16[4096,512]{1,0:T(8,128)(2,1)} %bitcast.15, bf16[4096,1024]{1,0:T(8,128)(2,1)} %all-gather.11.cloned.1.call-done), kind=kOutput, calls=%fused_computation.9 | convolution fusion | flops 4294967296 | bytes 14680064 | tf_op jit(solution)/shard_map/dot_general | solution.py:13
  768.9 15.6 %all-gather.9.cloned.1.call-done = bf16[4096,1024]{1,0:T(8,128)(2,1)} async-done(((bf16[512,1024]{1,0:T(8,128)(2,1)}), bf16[4096,1024]{1,0:T(8,128)(2,1)}) %all-gather.9.cloned.1.call-update) | async-done | bytes 8388624 | tf_op jit(solution)/shard_map/all_gather | solution.py:131
  784.4 8.2 convolution_bitcast_fusion.1
  792.7 2.5 pad_maximum_fusion
  795.1 19.7 %reduce-scatter.5.cloned.1.call-done = f32[128,19]{0,1:T(8,128)} async-done(((f32[1024,19]{0,1:T(8,128)}), f32[128,19]{0,1:T(8,128)}) %reduce-scatter.5.cloned.1.call-update) | async-done | bytes 9744 | tf_op jit(solution)/shard_map/reduce_scatter | solution.py:123
  (187 shorter events, 6.6 us)
Async XLA Ops:
  7.2 401.6 %copy-start = (bf16[1024,19]{0,1:T(8,128)(2,1)S(1)}, bf16[1024,19]{0,1:T(8,128)(2,1)}, u32[]{:S(2)}) copy-start(bf16[1024,19]{0,1:T(8,128)(2,1)} %param.14) | copy-start | bytes 116740
  13.2 6.5 copy-start.4
  13.2 6.5 copy-start.6
  13.2 190.4 %all-to-all-start.1 = ((bf16[8,512,1024]{2,1,0:T(8,128)(2,1)}), bf16[8,512,1024]{2,1,0:T(8,128)(2,1)}, u32[]{:S(2)}, u32[]{:S(2)}) async-start(bf16[8,512,1024]{2,1,0:T(8,128)(2,1)} %stack.15), calls=%async_computation.1 | async-start | bytes 16777216 | tf_op jit(solution)/shard_map/all_to_all | solution.py:88
  19.7 193.3 %all-gather.5.cloned.1.call-start = ((), (), s32[]{:S(2)}) async-start(), calls=%async_computation.6 | async-start | bytes 6553600 | tf_op jit(solution)/shard_map/all_gather | solution.py:100
  208.0 188.8 %all-to-all-start.2 = ((bf16[8,512,1024]{2,1,0:T(8,128)(2,1)}), bf16[8,512,1024]{2,1,0:T(8,128)(2,1)}, u32[]{:S(2)}, u32[]{:S(2)}) async-start(bf16[8,512,1024]{2,1,0:T(8,128)(2,1)} %stack.16), calls=%async_computation.2 | async-start | bytes 16777216 | tf_op jit(solution)/shard_map/all_to_all | solution.py:88
  213.0 183.9 %all-gather.7.cloned.1.call-start = ((), (), s32[]{:S(2)}) async-start(), calls=%async_computation.7 | async-start | bytes 6553600 | tf_op jit(solution)/shard_map/all_gather | solution.py:100
  213.0 10.9 %copy-start.5 = (f32[8,63,18]{1,0,2:T(8,128)S(1)}, f32[8,63,18]{1,0,2:T(8,128)}, u32[]{:S(2)}) copy-start(f32[8,63,18]{1,0,2:T(8,128)} %param.15) | copy-start | bytes 108868
  223.8 306.7 %reduce-scatter.3.cloned.1.call-start = ((), (), s32[]{:S(2)}) async-start(), calls=%async_computation.8 | async-start | bytes 10485760 | tf_op jit(solution)/shard_map/reduce_scatter | solution.py:135
  396.8 29.9 %copy-start.9 = (s32[8,63]{1,0:T(8,128)S(1)}, s32[8,63]{1,0:T(8,128)}, u32[]{:S(2)}) copy-start(s32[8,63]{1,0:T(8,128)} %param.16) | copy-start | bytes 6052
  396.8 29.9 %copy-start.7 = (s32[8,63]{1,0:T(8,128)S(1)}, s32[8,63]{1,0:T(8,128)}, u32[]{:S(2)}) copy-start(s32[8,63]{1,0:T(8,128)} %param.18) | copy-start | bytes 6052
  396.8 29.9 %copy-start.8 = (f32[8,63]{1,0:T(8,128)S(1)}, f32[8,63]{1,0:T(8,128)}, u32[]{:S(2)}) copy-start(f32[8,63]{1,0:T(8,128)} %param.17) | copy-start | bytes 6052
  407.7 1.1 copy-start.2
  447.2 313.3 %all-gather.11.cloned.1.call-start = ((), (), s32[]{:S(2)}) async-start(), calls=%async_computation.10 | async-start | bytes 9437184 | tf_op jit(solution)/shard_map/all_gather | solution.py:131
  459.0 134.9 %all-to-all-start = ((bf16[512,8,512]{0,2,1:T(8,128)(2,1)}), bf16[512,8,512]{0,2,1:T(8,128)(2,1)}, u32[]{:S(2)}, u32[]{:S(2)}) async-start(bf16[512,8,512]{0,2,1:T(8,128)(2,1)} %bitcast.62), calls=%async_computation | async-start | bytes 8388608 | tf_op jit(solution)/shard_map/all_to_all | solution.py:128
  463.6 320.8 %all-gather.9.cloned.1.call-start = ((), (), s32[]{:S(2)}) async-start(), calls=%async_computation.9 | async-start | bytes 9437184 | tf_op jit(solution)/shard_map/all_gather | solution.py:131
  533.9 2.2 slice-start
  593.9 166.6 %all-to-all-start.3 = ((bf16[512,8,512]{2,0,1:T(8,128)(2,1)}), bf16[512,8,512]{2,0,1:T(8,128)(2,1)}, u32[]{:S(2)}, u32[]{:S(2)}) async-start(bf16[512,8,512]{2,0,1:T(8,128)(2,1)} %bitcast.63), calls=%async_computation.4 | async-start | bytes 8388608 | tf_op jit(solution)/shard_map/all_to_all | solution.py:128
  598.5 216.3 %reduce-scatter.5.cloned.1.call-start = ((), (), s32[]{:S(2)}) async-start(), calls=%async_computation.11 | async-start | bytes 110592 | tf_op jit(solution)/shard_map/reduce_scatter | solution.py:123
  598.6 7.3 copy-start.3
  784.4 30.4 %copy-start.1 = (bf16[1024,19]{0,1:T(8,128)(2,1)S(1)}, bf16[1024,19]{0,1:T(8,128)(2,1)}, u32[]{:S(2)}) copy-start(bf16[1024,19]{0,1:T(8,128)(2,1)} %param.14) | copy-start | bytes 116740
Sparse Core Ops, SparseCore 0:
  22.9 62.7 all-gather.4
  224.0 62.6 all-gather.6
  447.3 83.1 reduce-scatter.2
  532.0 156.2 all-gather.10
  689.7 94.6 all-gather.8
  787.1 27.6 reduce-scatter.4
